TPU v7x, 32 devices: a whole 2x2x4 slice. The times are simulated.
32 devices in a mesh: zero: 8 (over y, x, core), tp: 4 (over z).
Axes of the slice: x: 2, y: 2, z: 4, core: 2. Of those that a mesh axis runs over, the one named last changes fastest.
Arguments:
- weight_gate: bfloat16 [2560, 9728], P('zero', 'tp'), may hold values from -0.125 to 0.125
- low_gate: bfloat16 [2560, 16], P('zero'), may hold values from -0.125 to 0.125
- high_gate: bfloat16 [16, 9728], P(None, 'tp'), may hold values from -1.5 to 1.5
- weight_up: bfloat16 [2560, 9728], P('zero', 'tp'), may hold values from -0.125 to 0.125
- low_up: bfloat16 [2560, 16], P('zero'), may hold values from -0.125 to 0.125
- high_up: bfloat16 [16, 9728], P(None, 'tp'), may hold values from -1.5 to 1.5
- weight_down: bfloat16 [9728, 2560], P('tp', 'zero'), may hold values from -0.0625 to 0.0625
- low_down: bfloat16 [9728, 16], P('tp'), may hold values from -0.0625 to 0.0625
- high_down: bfloat16 [16, 2560], P(None, 'zero'), may hold values from -1.5 to 1.5
- norm_train: float32 [2560], P(('zero', 'tp')), may hold values from 0.25 to 1.75
- norm_step: float32 [2560], P(('zero', 'tp')), may hold values from -0.3 to 0.3
Outputs:
- ready_gate: bfloat16 [2560, 9728], P(None, 'tp')
- ready_up: bfloat16 [2560, 9728], P(None, 'tp')
- ready_down: bfloat16 [9728, 2560], P('tp')
- serve_norm: bfloat16 [2560], replicated
All inputs are finite; a program needn't handle non-finite values.
Results may differ from a plain program's by a relative error of at most 0.001.
Values may be sent and summed in bfloat16 or wider, within the bound.
A program may use at most 128 MiB of HBM per device.

v0:
```python
import jax
import jax.numpy as jnp
from jax import lax
from jax.sharding import PartitionSpec as P

mix_rate = 0.5


def local(
    weight_gate,
    low_gate,
    high_gate,
    weight_up,
    low_up,
    high_up,
    weight_down,
    low_down,
    high_down,
    norm_train,
    norm_step,
):
    moved_gate, moved_up, moved_down, factor_gate, factor_up, factor_down = (
        lax.all_gather(weight_gate, "zero", axis=0, tiled=True),
        lax.all_gather(weight_up, "zero", axis=0, tiled=True),
        lax.all_gather(weight_down, "zero", axis=1, tiled=True),
        lax.all_gather(low_gate, "zero", axis=0, tiled=True),
        lax.all_gather(low_up, "zero", axis=0, tiled=True),
        lax.all_gather(high_down, "zero", axis=1, tiled=True),
    )
    latest_gate = moved_gate.astype(jnp.float32) + mix_rate * jnp.dot(
        factor_gate, high_gate, preferred_element_type=jnp.float32
    )
    ready_gate = latest_gate.astype(jnp.bfloat16)
    latest_up = moved_up.astype(jnp.float32) + mix_rate * jnp.dot(
        factor_up, high_up, preferred_element_type=jnp.float32
    )
    ready_up = latest_up.astype(jnp.bfloat16)
    latest_down = moved_down.astype(jnp.float32) + mix_rate * jnp.dot(
        low_down, factor_down, preferred_element_type=jnp.float32
    )
    ready_down = latest_down.astype(jnp.bfloat16)
    serve_norm = lax.all_gather(
        (norm_train + norm_step).astype(jnp.bfloat16), ("zero", "tp"), axis=0, tiled=True
    )
    return (ready_gate, ready_up, ready_down, serve_norm)


def solution(mesh):
    return jax.shard_map(
        local,
        mesh=mesh,
        in_specs=(
            P("zero", "tp"),
            P("zero", None),
            P(None, "tp"),
            P("zero", "tp"),
            P("zero", None),
            P(None, "tp"),
            P("tp", "zero"),
            P("tp", None),
            P(None, "zero"),
            P(("zero", "tp")),
            P(("zero", "tp")),
        ),
        out_specs=(P(None, "tp"), P(None, "tp"), P("tp", None), P()),
        check_vma=False,
    )
```

profile of v0, /device:TPU:0, one launch (start us, length us, event | category | flops | bytes accessed | tf_op | source)
XLA Modules:
  0.0 248.3 jit_solution(13862826156925674627)
XLA Ops:
  7.2 0.0 copy-start
  7.2 0.0 all-gather.11.cloned.1.call-start
  7.2 0.7 all-gather.11.cloned.1.call-update
  7.9 0.0 all-gather.7.cloned.1.call-start
  8.0 0.7 all-gather.7.cloned.1.call-update
  8.7 0.0 all-gather.9.cloned.1.call-start
  8.7 0.7 all-gather.9.cloned.1.call-update
  9.4 10.9 %all-gather = bf16[8,320,16]{1,2,0:T(8,128)(2,1)S(1)} all-gather(bf16[1,320,16]{1,2,0:T(8,128)(2,1)} %bitcast.17), channel_id=1, replica_groups=mesh['zero'=8,'tp'=4] {'zero'}, dimensions={0}, use_global_device_ids=true | all-gather | bytes 92160 | tf_op jit(solution)/shard_map/all_gather | solution.py:26
  20.3 0.1 reshape.11
  20.4 9.6 %all-gather.1 = bf16[8,320,16]{1,2,0:T(8,128)(2,1)S(1)} all-gather(bf16[1,320,16]{1,2,0:T(8,128)(2,1)} %bitcast.18), channel_id=1, replica_groups=mesh['zero'=8,'tp'=4] {'zero'}, dimensions={0}, use_global_device_ids=true | all-gather | bytes 92160 | tf_op jit(solution)/shard_map/all_gather | solution.py:27
  30.0 0.1 reshape.13
  30.1 9.0 %all-gather.2 = bf16[8,320,16]{1,2,0:T(8,128)(2,1)S(1)} all-gather(bf16[1,320,16]{1,2,0:T(8,128)(2,1)} %bitcast.19), channel_id=1, replica_groups=mesh['zero'=8,'tp'=4] {'zero'}, dimensions={0}, use_global_device_ids=true | all-gather | bytes 92160 | tf_op jit(solution)/shard_map/all_gather | solution.py:28
  39.2 0.1 reshape.15
  39.3 0.7 add_convert_fusion.3
  40.0 0.2 dynamic-update-slice
  40.2 40.8 %all-reduce = bf16[2560]{0:T(1024)(128)(2,1)} all-reduce(bf16[2560]{0:T(1024)(128)(2,1)S(1)} %dynamic-update-slice), channel_id=1, replica_groups=mesh['zero'=8,'tp'=4] {'zero','tp'}, use_global_device_ids=true, to_apply=%add | all-reduce | flops 2560 | bytes 10240
  81.0 4.8 %all-gather.11.cloned.1.call-done = bf16[2432,2560]{0,1:T(8,128)(2,1)} async-done(((bf16[2432,320]{0,1:T(8,128)(2,1)}), bf16[2432,2560]{0,1:T(8,128)(2,1)}) %all-gather.11.cloned.1.call-update) | async-done | bytes 12451856 | tf_op jit(solution)/shard_map/all_gather | solution.py:25
  85.8 17.3 %copy.22 = bf16[2432,2560]{1,0:T(8,128)(2,1)} copy(bf16[2432,2560]{0,1:T(8,128)(2,1)} %all-gather.11.cloned.1.call-done) | data formatting | bytes 24903680 | tf_op jit(solution)/shard_map/all_gather | solution.py:25
  103.0 0.0 copy-done
  103.0 0.0 copy-start.2
  103.0 9.4 %add_convert_fusion = bf16[2432,2560]{1,0:T(8,128)(2,1)} fusion(bf16[2432,2560]{1,0:T(8,128)(2,1)} %copy.22, bf16[2432,16]{0,1:T(8,128)(2,1)S(1)} %copy-done, bf16[2560,16]{0,1:T(8,128)(2,1)S(1)} %reshape.15), kind=kOutput, calls=%fused_computation | convolution fusion | flops 224133120 | bytes 25063424 | tf_op jit(solution)/shard_map/dot_general | solution.py:38
  112.4 0.0 copy-start.3
  112.4 46.7 %all-gather.7.cloned.1.call-done = bf16[2560,2432]{1,0:T(8,128)(2,1)} async-done(((bf16[320,2432]{1,0:T(8,128)(2,1)}), bf16[2560,2432]{1,0:T(8,128)(2,1)}) %all-gather.7.cloned.1.call-update) | async-done | bytes 12451856 | tf_op jit(solution)/shard_map/all_gather | solution.py:23
  159.1 0.0 copy-done.2
  159.1 0.0 copy-start.1
  159.1 9.4 %add_convert_fusion.2 = bf16[2560,2432]{1,0:T(8,128)(2,1)} fusion(bf16[2560,2432]{1,0:T(8,128)(2,1)} %all-gather.7.cloned.1.call-done, bf16[2560,16]{0,1:T(8,128)(2,1)S(1)} %reshape.11, bf16[16,2432]{1,0:T(8,128)(2,1)S(1)} %copy-done.2), kind=kOutput, calls=%fused_computation.2 | convolution fusion | flops 224133120 | bytes 25063424 | tf_op jit(solution)/shard_map/dot_general | solution.py:30
  168.4 64.0 %all-gather.9.cloned.1.call-done = bf16[2560,2432]{1,0:T(8,128)(2,1)} async-done(((bf16[320,2432]{1,0:T(8,128)(2,1)}), bf16[2560,2432]{1,0:T(8,128)(2,1)}) %all-gather.9.cloned.1.call-update) | async-done | bytes 12451856 | tf_op jit(solution)/shard_map/all_gather | solution.py:24
  232.4 0.0 copy-done.3
  232.4 9.3 %add_convert_fusion.1 = bf16[2560,2432]{1,0:T(8,128)(2,1)} fusion(bf16[2560,2432]{1,0:T(8,128)(2,1)} %all-gather.9.cloned.1.call-done, bf16[2560,16]{0,1:T(8,128)(2,1)S(1)} %reshape.13, bf16[16,2432]{1,0:T(8,128)(2,1)S(1)} %copy-done.3), kind=kOutput, calls=%fused_computation.1 | convolution fusion | flops 224133120 | bytes 25063424 | tf_op jit(solution)/shard_map/dot_general | solution.py:34
  241.8 0.0 copy-done.1
  (4 shorter events, 0.1 us)
Async XLA Ops:
  7.2 95.9 %copy-start = (bf16[2432,16]{0,1:T(8,128)(2,1)S(1)}, bf16[2432,16]{0,1:T(8,128)(2,1)}, u32[]{:S(2)}) copy-start(bf16[2432,16]{0,1:T(8,128)(2,1)} %param.18) | copy-start | bytes 233476
  7.2 78.6 %all-gather.11.cloned.1.call-start = ((), (), s32[]{:S(2)}) async-start(), calls=%async_computation.2 | async-start | bytes 14008320 | tf_op jit(solution)/shard_map/all_gather | solution.py:25
  7.9 151.1 %all-gather.7.cloned.1.call-start = ((), (), s32[]{:S(2)}) async-start(), calls=%async_computation | async-start | bytes 14008320 | tf_op jit(solution)/shard_map/all_gather | solution.py:23
  8.7 223.8 %all-gather.9.cloned.1.call-start = ((), (), s32[]{:S(2)}) async-start(), calls=%async_computation.1 | async-start | bytes 14008320 | tf_op jit(solution)/shard_map/all_gather | solution.py:24
  103.0 56.0 %copy-start.2 = (bf16[16,2432]{1,0:T(8,128)(2,1)S(1)}, bf16[16,2432]{1,0:T(8,128)(2,1)}, u32[]{:S(2)}) copy-start(bf16[16,2432]{1,0:T(8,128)(2,1)} %param.13) | copy-start | bytes 233476
  112.4 120.0 %copy-start.3 = (bf16[16,2432]{1,0:T(8,128)(2,1)S(1)}, bf16[16,2432]{1,0:T(8,128)(2,1)}, u32[]{:S(2)}) copy-start(bf16[16,2432]{1,0:T(8,128)(2,1)} %param.16) | copy-start | bytes 233476
  159.1 82.7 %copy-start.1 = (bf16[2432,16]{0,1:T(8,128)(2,1)S(1)}, bf16[2432,16]{0,1:T(8,128)(2,1)}, u32[]{:S(2)}) copy-start(bf16[2432,16]{0,1:T(8,128)(2,1)} %param.18) | copy-start | bytes 233476
Sparse Core Ops, SparseCore 0:
  9.9 75.8 all-gather.10
  87.6 71.3 all-gather.6
  161.0 71.4 all-gather.8
where the time goes:
time: 249 us; the launch traced here: 248 us
  waiting for transfers between devices  117 us (47%)
  blocking collectives  70.3 us (28%)
  matrix products  28.1 us (11%)
  local copies, waits for them, and re-layouts  17.9 us (7%)
  between operations  13.8 us (6%)
    all_gather x1, waiting for transfers between devices, local(): lax.all_gather(weight_up, 'zero', axis=0, tiled=True)  64 us
    all_gather x1, waiting for transfers between devices, local(): lax.all_gather(weight_gate, 'zero', axis=0, tiled=True)  46.7 us
    unnamed x1, blocking collectives  40.8 us
    all_gather x1, local copies, waits for them, and re-layouts, local(): lax.all_gather(weight_down, 'zero', axis=1, tiled=True)  17.3 us
    all_gather x1, blocking collectives, local(): lax.all_gather(low_gate, 'zero', axis=0, tiled=True)  10.9 us
    all_gather x1, blocking collectives, local(): lax.all_gather(low_up, 'zero', axis=0, tiled=True)  9.56 us
    dot_general x1, matrix products, local(): jnp.dot(low_down, factor_down, preferred_element_type=jnp.float32)  9.37 us
    dot_general x1, matrix products, local(): jnp.dot(factor_gate, high_gate, preferred_element_type=jnp.float32)  9.36 us
  transfers between devices with their start and end apart: 3, of which 3 were waited for; matrix products, arithmetic and copies ran while one was open for 15% of the time, Pallas kernels for 0%

commit v1 on v0

--- a/solution.py
+++ b/solution.py
@@ -22,7 +22,7 @@
     moved_gate, moved_up, moved_down, factor_gate, factor_up, factor_down = (
         lax.all_gather(weight_gate, "zero", axis=0, tiled=True),
         lax.all_gather(weight_up, "zero", axis=0, tiled=True),
-        lax.all_gather(weight_down, "zero", axis=1, tiled=True),
+        jnp.concatenate(lax.all_gather(weight_down, "zero"), axis=1),
         lax.all_gather(low_gate, "zero", axis=0, tiled=True),
         lax.all_gather(low_up, "zero", axis=0, tiled=True),
         lax.all_gather(high_down, "zero", axis=1, tiled=True),

time: 249 us -> 249 us (level)
  waiting for transfers between devices: 117 us -> 62.6 us
  local copies, waits for them, and re-layouts: 17.9 us -> 59.8 us
  other arithmetic: 0.68 us -> 7.72 us
  matrix products: 28.1 us -> 33.9 us
    all_gather x1, waiting for transfers between devices: 64 us -> 7.09 us  [local(): lax.all_gather(weight_up, 'zero', axis=0, tiled=True)]
    convert_element_type x0 -> x2, local copies, waits for them, and re-layouts: none -> 49.2 us  [local(): moved_down.astype(jnp.float32)]
    all_gather x1 -> x0, local copies, waits for them, and re-layouts: 17.3 us -> none  [local(): lax.all_gather(weight_down, 'zero', axis=1, tiled=True)]
    unnamed x13 -> x12, local copies, waits for them, and re-layouts: 0.59 us -> 10.6 us
    convert_element_type x0 -> x1, other arithmetic: none -> 7.04 us  [local(): moved_down.astype(jnp.float32)]
    dot_general x1, matrix products: 9.37 us -> 15.3 us  [local(): jnp.dot(low_down, factor_down, preferred_element_type=jnp.float32)]
  transfers between devices with their start and end apart: 3 -> 3, of which waited for: 3 -> 3; matrix products, arithmetic and copies ran while one was open for 15% -> 37% of each run, Pallas kernels for 0% -> 0%
where the time goes in v1:
time: 249 us; the launch traced here: 248 us
  blocking collectives  70.3 us (28%)
  waiting for transfers between devices  62.6 us (25%)
  local copies, waits for them, and re-layouts  59.8 us (24%)
  matrix products  33.9 us (14%)
  between operations  13.8 us (6%)
  other arithmetic  7.72 us (3%)
    convert_element_type x2, local copies, waits for them, and re-layouts, local(): moved_down.astype(jnp.float32)  49.2 us
    all_gather x1, waiting for transfers between devices, local(): lax.all_gather(weight_gate, 'zero', axis=0, tiled=True)  48.8 us
    unnamed x1, blocking collectives  40.8 us
    dot_general x1, matrix products, local(): jnp.dot(low_down, factor_down, preferred_element_type=jnp.float32)  15.3 us
    all_gather x1, blocking collectives, local(): lax.all_gather(high_down, 'zero', axis=1, tiled=True)  10.9 us
    unnamed x12, local copies, waits for them, and re-layouts  10.6 us
    all_gather x1, blocking collectives, local(): lax.all_gather(low_up, 'zero', axis=0, tiled=True)  9.56 us
    dot_general x1, matrix products, local(): jnp.dot(factor_up, high_up, preferred_element_type=jnp.float32)  9.33 us
  transfers between devices with their start and end apart: 3, of which 3 were waited for; matrix products, arithmetic and copies ran while one was open for 37% of the time, Pallas kernels for 0%

profile of v1, /device:TPU:0, one launch (start us, length us, event | category | flops | bytes accessed | tf_op | source)
XLA Modules:
  0.0 248.2 jit_solution(7973017726759519328)
XLA Ops:
  7.2 0.0 copy-start
  7.2 0.0 all-gather.12.cloned.1.call-start
  7.2 0.7 all-gather.12.cloned.1.call-update
  7.9 0.0 all-gather.10.cloned.1.call-start
  8.0 0.7 all-gather.10.cloned.1.call-update
  8.7 0.0 all-gather.8.cloned.1.call-start
  8.7 0.7 all-gather.8.cloned.1.call-update
  9.4 10.9 %all-gather.3 = bf16[8,320,16]{1,2,0:T(8,128)(2,1)S(1)} all-gather(bf16[1,320,16]{1,2,0:T(8,128)(2,1)} %bitcast.27), channel_id=1, replica_groups=mesh['zero'=8,'tp'=4] {'zero'}, dimensions={0}, use_global_device_ids=true | all-gather | bytes 92160 | tf_op jit(solution)/shard_map/all_gather | solution.py:28
  20.3 0.1 reshape.22
  20.4 9.6 %all-gather.2 = bf16[8,320,16]{1,2,0:T(8,128)(2,1)S(1)} all-gather(bf16[1,320,16]{1,2,0:T(8,128)(2,1)} %bitcast.28), channel_id=1, replica_groups=mesh['zero'=8,'tp'=4] {'zero'}, dimensions={0}, use_global_device_ids=true | all-gather | bytes 92160 | tf_op jit(solution)/shard_map/all_gather | solution.py:27
  30.0 0.1 reshape.20
  30.1 9.0 %all-gather.1 = bf16[8,320,16]{1,2,0:T(8,128)(2,1)S(1)} all-gather(bf16[1,320,16]{1,2,0:T(8,128)(2,1)} %bitcast.29), channel_id=1, replica_groups=mesh['zero'=8,'tp'=4] {'zero'}, dimensions={0}, use_global_device_ids=true | all-gather | bytes 92160 | tf_op jit(solution)/shard_map/all_gather | solution.py:26
  39.2 0.1 reshape.18
  39.3 0.7 add_convert_fusion.3
  40.0 0.2 dynamic-update-slice
  40.2 40.8 %all-reduce = bf16[2560]{0:T(1024)(128)(2,1)} all-reduce(bf16[2560]{0:T(1024)(128)(2,1)S(1)} %dynamic-update-slice), channel_id=1, replica_groups=mesh['zero'=8,'tp'=4] {'zero','tp'}, use_global_device_ids=true, to_apply=%add | all-reduce | flops 2560 | bytes 10240
  81.0 4.6 %all-gather.12.cloned.1.call-done = bf16[19456,320]{0,1:T(8,128)(2,1)} async-done(((bf16[2432,320]{0,1:T(8,128)(2,1)}), bf16[19456,320]{0,1:T(8,128)(2,1)}) %all-gather.12.cloned.1.call-update) | async-done | bytes 12451856 | tf_op jit(solution)/shard_map/all_gather | solution.py:25
  85.7 7.0 %convert_element_type.38 = f32[19456,320]{0,1:T(8,128)S(1)} convert(bf16[19456,320]{0,1:T(8,128)(2,1)} %all-gather.12.cloned.1.call-done) | non-fusion elementwise | flops 6225920 | bytes 37355520 | tf_op jit(solution)/shard_map/convert_element_type | solution.py:38
  92.7 10.0 %copy.30 = f32[40,8,8,2432]{3,2,1,0:T(8,128)} copy(f32[40,8,8,2432]{3,1,2,0:T(8,128)S(1)} %bitcast.24) | data formatting | bytes 49807360
  102.7 22.2 %copy.27 = f32[2432,8,320]{0,2,1:T(8,128)} copy(f32[2432,8,320]{0,1,2:T(8,128)} %bitcast.25) | data formatting | bytes 49807360 | tf_op jit(solution)/shard_map/convert_element_type | solution.py:38
  125.0 26.9 %copy.29 = f32[2432,2560]{1,0:T(8,128)} copy(f32[2432,2560]{0,1:T(8,128)} %bitcast.26) | data formatting | bytes 49807360 | tf_op jit(solution)/shard_map/convert_element_type | solution.py:38
  151.9 0.0 copy-start.1
  151.9 7.1 %all-gather.10.cloned.1.call-done = bf16[2560,2432]{1,0:T(8,128)(2,1)} async-done(((bf16[320,2432]{1,0:T(8,128)(2,1)}), bf16[2560,2432]{1,0:T(8,128)(2,1)}) %all-gather.10.cloned.1.call-update) | async-done | bytes 12451856 | tf_op jit(solution)/shard_map/all_gather | solution.py:24
  159.0 0.0 copy-done
  159.0 9.3 %add_convert_fusion.1 = bf16[2560,2432]{1,0:T(8,128)(2,1)} fusion(bf16[2560,2432]{1,0:T(8,128)(2,1)} %all-gather.10.cloned.1.call-done, bf16[2560,16]{0,1:T(8,128)(2,1)S(1)} %reshape.20, bf16[16,2432]{1,0:T(8,128)(2,1)S(1)} %copy-done), kind=kOutput, calls=%fused_computation.1 | convolution fusion | flops 224133120 | bytes 25063424 | tf_op jit(solution)/shard_map/dot_general | solution.py:34
  168.3 0.0 copy-done.1
  168.3 0.0 copy-start.2
  168.3 15.3 %add_convert_fusion = bf16[2432,2560]{1,0:T(8,128)(2,1)} fusion(f32[2432,2560]{1,0:T(8,128)} %copy.29, bf16[2432,16]{0,1:T(8,128)(2,1)S(1)} %copy-done.1, bf16[2560,16]{0,1:T(8,128)(2,1)S(1)} %reshape.22), kind=kOutput, calls=%fused_computation | convolution fusion | flops 217907200 | bytes 37515264 | tf_op jit(solution)/shard_map/dot_general | solution.py:38
  183.6 48.8 %all-gather.8.cloned.1.call-done = bf16[2560,2432]{1,0:T(8,128)(2,1)} async-done(((bf16[320,2432]{1,0:T(8,128)(2,1)}), bf16[2560,2432]{1,0:T(8,128)(2,1)}) %all-gather.8.cloned.1.call-update) | async-done | bytes 12451856 | tf_op jit(solution)/shard_map/all_gather | solution.py:23
  232.3 0.0 copy-done.2
  232.3 9.3 %add_convert_fusion.2 = bf16[2560,2432]{1,0:T(8,128)(2,1)} fusion(bf16[2560,2432]{1,0:T(8,128)(2,1)} %all-gather.8.cloned.1.call-done, bf16[2560,16]{0,1:T(8,128)(2,1)S(1)} %reshape.18, bf16[16,2432]{1,0:T(8,128)(2,1)S(1)} %copy-done.2), kind=kOutput, calls=%fused_computation.2 | convolution fusion | flops 224133120 | bytes 25063424 | tf_op jit(solution)/shard_map/dot_general | solution.py:30
  (4 shorter events, 0.1 us)
Async XLA Ops:
  7.2 151.8 %copy-start = (bf16[16,2432]{1,0:T(8,128)(2,1)S(1)}, bf16[16,2432]{1,0:T(8,128)(2,1)}, u32[]{:S(2)}) copy-start(bf16[16,2432]{1,0:T(8,128)(2,1)} %param.16) | copy-start | bytes 233476
  7.2 78.5 %all-gather.12.cloned.1.call-start = ((), (), s32[]{:S(2)}) async-start(), calls=%async_computation.2 | async-start | bytes 14008320 | tf_op jit(solution)/shard_map/all_gather | solution.py:25
  7.9 151.1 %all-gather.10.cloned.1.call-start = ((), (), s32[]{:S(2)}) async-start(), calls=%async_computation.1 | async-start | bytes 14008320 | tf_op jit(solution)/shard_map/all_gather | solution.py:24
  8.7 223.7 %all-gather.8.cloned.1.call-start = ((), (), s32[]{:S(2)}) async-start(), calls=%async_computation | async-start | bytes 14008320 | tf_op jit(solution)/shard_map/all_gather | solution.py:23
  151.9 16.4 %copy-start.1 = (bf16[2432,16]{0,1:T(8,128)(2,1)S(1)}, bf16[2432,16]{0,1:T(8,128)(2,1)}, u32[]{:S(2)}) copy-start(bf16[2432,16]{0,1:T(8,128)(2,1)} %param.18) | copy-start | bytes 233476
  168.3 64.0 %copy-start.2 = (bf16[16,2432]{1,0:T(8,128)(2,1)S(1)}, bf16[16,2432]{1,0:T(8,128)(2,1)}, u32[]{:S(2)}) copy-start(bf16[16,2432]{1,0:T(8,128)(2,1)} %param.13) | copy-start | bytes 233476
Sparse Core Ops, SparseCore 0:
  9.9 75.7 all-gather.11
  87.6 71.3 all-gather.9
  160.9 71.4 all-gather.7
